TPU v7x, 32 devices: a whole 2x2x4 slice. The times are simulated.
32 devices in a mesh: dp: 4 (over z), tensor: 8 (over y, x, core).
Axes of the slice: x: 2, y: 2, z: 4, core: 2. Of those that a mesh axis runs over, the one named last changes fastest.
Arguments:
- activations: bfloat16 [1024, 27648], P('dp', 'tensor'), may hold values from -6 to 6
- left_factor: float32 [216, 216], replicated, may hold values from -2 to 3, as said below
- right_factor: float32 [128, 128], replicated, may hold values from -2 to 3, as said below
- clip_scale: float32 [128, 216], replicated, may hold values from 0.5 to 3
- weight_rows: bfloat16 [27648, 5120], P('tensor'), may hold values from -0.0390625 to 0.0390625
- target: bfloat16 [1024, 5120], P('dp'), may hold values from -6 to 6
Outputs:
- grad_left: float32 [216, 216], replicated
- grad_right: float32 [128, 128], replicated
- grad_input: float32 [1024, 27648], P('dp', 'tensor')
Inputs may be any that keep to these rules, and one draw needn't show every extreme that they name: `left_factor`: the identity plus independent entries of order one over the square root of 216. `right_factor`: the identity plus independent entries of order one over the square root of 128.
All inputs are finite; a program needn't handle non-finite values.
Results may differ from a plain program's by a relative error of at most 0.007.
Values may be sent and summed in bfloat16 or wider, within the bound.
A program may use at most 128 MiB of HBM per device.

v0:
```python
import jax
import jax.numpy as jnp
from jax import lax
from jax.sharding import PartitionSpec as P


def local(activations, left_factor, right_factor, clip_scale, weight_rows, target):
    highest = lax.Precision.HIGHEST
    tok_rows = activations.shape[0]
    width_left = left_factor.shape[0]
    local_right = activations.shape[1] // width_left
    inputs = activations.reshape(tok_rows, local_right, width_left)
    moved = lax.all_to_all(inputs, "tensor", split_axis=0, concat_axis=1, tiled=True)
    mixed = jnp.einsum("tji,ik->tjk", moved.astype(jnp.float32), left_factor, precision=highest)
    rotated = jnp.einsum("jl,tjk->tlk", right_factor, mixed, precision=highest)
    bounded = jnp.tanh(rotated / clip_scale)
    clipped = (clip_scale * bounded).astype(jnp.bfloat16)
    clipped_back = lax.all_to_all(clipped, "tensor", split_axis=1, concat_axis=0, tiled=True)
    partial_out = jnp.dot(
        clipped_back.reshape(tok_rows, -1), weight_rows, preferred_element_type=jnp.float32
    )
    total = lax.psum(partial_out, "tensor")
    out_grad = (total - target.astype(jnp.float32)).astype(jnp.bfloat16)
    clipped_grad = lax.dot_general(
        out_grad, weight_rows, (((1,), (1,)), ((), ())), preferred_element_type=jnp.float32
    )
    clipped_grad = clipped_grad.reshape(tok_rows, local_right, width_left)
    grad_owned = lax.all_to_all(clipped_grad, "tensor", split_axis=0, concat_axis=1, tiled=True)
    rotated_grad = grad_owned * (1.0 - bounded * bounded)
    mixed_grad = jnp.einsum("jl,tlk->tjk", right_factor, rotated_grad, precision=highest)
    right_part = jnp.einsum("tjk,tlk->jl", mixed, rotated_grad, precision=highest)
    grad_back = lax.all_to_all(mixed_grad, "tensor", split_axis=1, concat_axis=0, tiled=True)
    input_grad = jnp.einsum("tjk,ik->tji", grad_back, left_factor, precision=highest).reshape(
        tok_rows, -1
    )
    left_part = jnp.einsum("tji,tjk->ik", inputs.astype(jnp.float32), grad_back, precision=highest)
    left_sum, right_sum = lax.psum((left_part, right_part), ("dp", "tensor"))
    return (left_sum, right_sum, input_grad)


def solution(mesh):
    placed = (P("dp", "tensor"), P(), P(), P(), P("tensor", None), P("dp", None))
    return jax.shard_map(
        local, mesh=mesh, in_specs=placed, out_specs=(P(), P(), P("dp", "tensor")), check_vma=False
    )
```

profile of v0, /device:TPU:8, one launch (start us, length us, event | category | flops | bytes accessed | tf_op | source)
XLA Modules:
  0.0 508.3 jit_solution(451690624203319944)
XLA Ops:
  7.2 0.0 copy-start
  7.2 0.0 all-reduce.4.cloned.1.call-start
  7.2 2.7 copy.31
  9.9 3.0 copy.32
  12.9 30.3 %all_to_all.69 = bf16[256,16,216]{2,1,0:T(8,128)(2,1)S(1)} all-to-all(bf16[256,16,216]{2,1,0:T(8,128)(2,1)} %copy.32), channel_id=1, replica_groups=mesh['dp'=4,'tensor'=8] {'tensor'}, dimensions={0} | all-to-all | bytes 3538944 | tf_op jit(solution)/shard_map/all_to_all | solution.py:13
  43.2 0.3 copy.33
  43.5 0.0 copy-start.2
  43.5 0.0 copy-start.3
  43.5 0.0 copy-done
  43.5 2.1 fusion.6
  45.7 0.0 copy-done.2
  45.7 0.0 copy-done.3
  45.7 0.0 copy-start.1
  45.7 4.7 multiply_convert_fusion
  50.4 0.0 copy-done.1
  50.4 4.5 copy.36
  54.9 30.1 %all_to_all.70 = bf16[32,128,216]{2,0,1:T(8,128)(2,1)S(1)} all-to-all(bf16[32,128,216]{2,0,1:T(8,128)(2,1)} %copy.36), channel_id=1, replica_groups=mesh['dp'=4,'tensor'=8] {'tensor'}, dimensions={1} | all-to-all | bytes 3538944 | tf_op jit(solution)/shard_map/all_to_all | solution.py:18
  85.0 2.6 copy.38
  87.6 5.2 %reshape.21 = bf16[256,3456]{1,0:T(8,128)(2,1)} reshape(bf16[8,32,16,216]{3,2,1,0:T(8,128)(2,1)} %copy.38) | data formatting | bytes 3538944 | tf_op jit(solution)/shard_map/reshape | solution.py:20
  92.8 18.0 %fusion.12 = f32[256,5120]{1,0:T(8,128)} fusion(bf16[256,3456]{1,0:T(8,128)(2,1)} %reshape.21, bf16[3456,5120]{1,0:T(8,128)(2,1)} %param.10), kind=kOutput, calls=%fused_computation.18 | convolution fusion | flops 9059696640 | bytes 42401792 | tf_op jit(solution)/shard_map/dot_general | solution.py:19
  110.8 0.0 all-reduce.4.cloned.1.call-update
  110.8 91.8 %all-reduce.4.cloned.1.call-done = f32[256,5120]{1,0:T(8,128)} async-done(((f32[256,5120]{1,0:T(8,128)}), f32[256,5120]{1,0:T(8,128)}) %all-reduce.4.cloned.1.call-update) | async-done | bytes 5242896 | tf_op jit(solution)/shard_map/psum | solution.py:22
  202.6 19.4 %fusion.1 = f32[256,3456]{0,1:T(8,128)} fusion(bf16[3456,5120]{1,0:T(8,128)(2,1)} %param.10, f32[256,5120]{1,0:T(8,128)} %all-reduce.4.cloned.1.call-done, bf16[256,5120]{1,0:T(8,128)(2,1)} %param.11), kind=kOutput, calls=%fused_computation.5 | convolution fusion | flops 9063628800 | bytes 46792704 | tf_op jit(solution)/shard_map/dot_general | solution.py:24
  222.0 5.3 %copy.40 = f32[256,16,216]{2,1,0:T(8,128)} copy(f32[256,16,216]{0,2,1:T(8,128)} %bitcast.63) | data formatting | bytes 7077888 | tf_op jit(solution)/shard_map/reshape | solution.py:27
  227.3 52.6 %all_to_all.71 = f32[256,16,216]{2,1,0:T(8,128)S(1)} all-to-all(f32[256,16,216]{2,1,0:T(8,128)} %copy.40), channel_id=1, replica_groups=mesh['dp'=4,'tensor'=8] {'tensor'}, dimensions={0} | all-to-all | bytes 7077888 | tf_op jit(solution)/shard_map/all_to_all | solution.py:28
  279.9 2.7 copy.41
  282.6 5.5 %copy.42 = f32[32,128,216]{1,2,0:T(8,128)} copy(f32[32,128,216]{2,1,0:T(8,128)} %bitcast.55) | data formatting | bytes 7077888 | tf_op jit(solution)/shard_map/all_to_all | solution.py:28
  288.1 6.4 %convolution_bitcast_fusion = f32[32,128,216]{1,2,0:T(8,128)} fusion(f32[32,128,216]{1,2,0:T(8,128)} %copy.42, f32[32,128,216]{1,2,0:T(8,128)} %get-tuple-element.15, f32[128,128]{1,0:T(8,128)S(1)} %copy-done.2), kind=kOutput, calls=%fused_computation.6 | convolution fusion | flops 1361608704 | bytes 10682368 | tf_op jit(solution)/shard_map/jl,tlk->tjk/dot_general | solution.py:30
  294.5 5.3 %copy.43 = f32[32,128,216]{2,0,1:T(8,128)} copy(f32[32,128,216]{1,2,0:T(8,128)} %convolution_bitcast_fusion) | data formatting | bytes 7077888 | tf_op jit(solution)/shard_map/jl,tlk->tjk/transpose | solution.py:30
  299.7 4.6 all-to-all-start.3
  304.3 0.3 all-reduce.6.cloned.1.call-start
  304.5 10.7 %fusion.3 = f32[128,128]{1,0:T(8,128)} fusion(f32[32,128,216]{1,2,0:T(8,128)} %copy-done.1, f32[32,128,216]{1,2,0:T(8,128)} %copy.42, f32[32,128,216]{1,2,0:T(8,128)} %get-tuple-element.15), kind=kOutput, calls=%fused_computation.9 | convolution fusion | flops 1361608704 | bytes 10682368 | tf_op jit(solution)/shard_map/tjk,tlk->jl/dot_general | solution.py:31
  315.3 38.1 %all-to-all-done.3 = f32[32,128,216]{2,0,1:T(8,128)} async-done(((f32[32,128,216]{2,0,1:T(8,128)}), f32[32,128,216]{2,0,1:T(8,128)}, u32[]{:S(2)}, u32[]{:S(2)}) %all-to-all-start.3) | async-done | bytes 3538976 | tf_op jit(solution)/shard_map/all_to_all | solution.py:32
  353.4 6.5 %copy.45 = f32[8,32,16,216]{3,2,1,0:T(8,128)} copy(f32[8,32,16,216]{3,1,2,0:T(8,128)} %bitcast.17) | data formatting | bytes 7077888 | tf_op jit(solution)/shard_map/all_to_all | solution.py:32
  359.9 5.1 %copy.46 = f32[256,16,216]{0,2,1:T(8,128)} copy(f32[256,16,216]{2,1,0:T(8,128)} %bitcast.56) | data formatting | bytes 7077888 | tf_op jit(solution)/shard_map/all_to_all | solution.py:32
  365.0 4.6 convolution_bitcast_fusion.1
  369.6 0.0 all-reduce.6.cloned.1.call-update
  369.6 7.1 %fusion.4 = f32[256,16,216]{0,2,1:T(8,128)} fusion(f32[256,16,216]{0,2,1:T(8,128)} %copy.46, f32[216,216]{1,0:T(8,128)S(1)} %copy-done), kind=kOutput, calls=%fused_computation.10 | convolution fusion | flops 2293235712 | bytes 7264512 | tf_op jit(solution)/shard_map/tjk,ik->tji/dot_general | solution.py:33
  376.7 5.2 %copy.49 = f32[256,3456]{1,0:T(8,128)} copy(f32[256,3456]{0,1:T(8,128)} %bitcast.59) | data formatting | bytes 7077888
  381.9 116.3 %all-reduce.6.cloned.1.call-done = (f32[216,216]{0,1:T(8,128)}, f32[128,128]{1,0:T(8,128)}) async-done(((f32[216,216]{0,1:T(8,128)}, f32[128,128]{1,0:T(8,128)}), (f32[216,216]{0,1:T(8,128)}, f32[128,128]{1,0:T(8,128)})) %all-reduce.6.cloned.1.call-update) | async-done | bytes 252176 | tf_op jit(solution)/shard_map/psum | solution.py:37
  498.2 1.7 copy.48
  499.9 1.5 copy.59
Async XLA Ops:
  7.2 36.4 %copy-start = (f32[216,216]{1,0:T(8,128)S(1)}, f32[216,216]{1,0:T(8,128)}, u32[]{:S(2)}) copy-start(f32[216,216]{1,0:T(8,128)} %param.7) | copy-start | bytes 559876
  7.2 195.4 %all-reduce.4.cloned.1.call-start = ((), (), s32[]{:S(2)}) async-start(), calls=%async_computation.4 | async-start | bytes 10485760 | tf_op jit(solution)/shard_map/psum | solution.py:22
  43.5 2.2 copy-start.2
  43.5 2.2 copy-start.3
  45.7 4.7 copy-start.1
  299.7 53.7 %all-to-all-start.3 = ((f32[32,128,216]{2,0,1:T(8,128)}), f32[32,128,216]{2,0,1:T(8,128)}, u32[]{:S(2)}, u32[]{:S(2)}) async-start(f32[32,128,216]{2,0,1:T(8,128)} %copy.43), calls=%async_computation.3 | async-start | bytes 8388608 | tf_op jit(solution)/shard_map/all_to_all | solution.py:32
  304.3 193.9 %all-reduce.6.cloned.1.call-start = ((), (), s32[]{:S(2)}) async-start(), calls=%async_computation.5 | async-start | bytes 573440 | tf_op jit(solution)/shard_map/psum | solution.py:37
Sparse Core Ops, SparseCore 0:
  110.9 91.6 all-reduce.3
  369.7 128.4 all-reduce.5
where the time goes:
time: 510 us; the launch traced here: 508 us
  waiting for transfers between devices  246 us (48%)
  blocking collectives  113 us (22%)
  matrix products  72.9 us (14%)
  local copies, waits for them, and re-layouts  57 us (11%)
  between operations  14.1 us (3%)
    psum x1, waiting for transfers between devices, local(): left_sum, right_sum = lax.psum((left_part, right_part), ('dp', 'tensor'))  116 us
    psum x1, waiting for transfers between devices, local(): total = lax.psum(partial_out, 'tensor')  91.8 us
    all_to_all x1, blocking collectives, local(): lax.all_to_all(clipped_grad, 'tensor', split_axis=0, concat_axis=1, tiled...  52.6 us
    all_to_all x1, waiting for transfers between devices, local(): lax.all_to_all(mixed_grad, 'tensor', split_axis=1, concat_axis=0, tiled=T...  38.1 us
    all_to_all x1, blocking collectives, local(): lax.all_to_all(inputs, 'tensor', split_axis=0, concat_axis=1, tiled=True)  30.3 us
    all_to_all x1, blocking collectives, local(): lax.all_to_all(clipped, 'tensor', split_axis=1, concat_axis=0, tiled=True)  30.1 us
    dot_general x1, matrix products, local(): lax.dot_general(out_grad, weight_rows, (((1,), (1,)), ((), ())), preferre...  19.4 us
    dot_general x1, matrix products, local(): jnp.dot(clipped_back.reshape(tok_rows, -1), weight_rows, preferred_elemen...  18 us
  transfers between devices with their start and end apart: 3, of which 3 were waited for; matrix products, arithmetic and copies ran while one was open for 5% of the time, Pallas kernels for 0%

commit v1 on v0

--- a/solution.py
+++ b/solution.py
@@ -2,6 +2,7 @@
 import jax.numpy as jnp
 from jax import lax
 from jax.sharding import PartitionSpec as P
+from jax.lax import psum
 
 
 def local(activations, left_factor, right_factor, clip_scale, weight_rows, target):
@@ -34,7 +35,7 @@
         tok_rows, -1
     )
     left_part = jnp.einsum("tji,tjk->ik", inputs.astype(jnp.float32), grad_back, precision=highest)
-    left_sum, right_sum = lax.psum((left_part, right_part), ("dp", "tensor"))
+    left_sum, right_sum = psum(psum((left_part, right_part), "tensor"), "dp")
     return (left_sum, right_sum, input_grad)
 
 

time: 510 us -> 474 us (0.929)
  waiting for transfers between devices: 246 us -> 209 us
    psum x1 -> x2, waiting for transfers between devices: 116 us -> 78.8 us  [local(): left_sum, right_sum = psum(psum((left_part, right_part), 'tensor'), 'dp')]
  transfers between devices with their start and end apart: 3 -> 4, of which waited for: 3 -> 4; matrix products, arithmetic and copies ran while one was open for 5% -> 5% of each run, Pallas kernels for 0% -> 0%
where the time goes in v1:
time: 474 us; the launch traced here: 471 us
  waiting for transfers between devices  209 us (44%)
  blocking collectives  113 us (24%)
  matrix products  73 us (15%)
  local copies, waits for them, and re-layouts  57.1 us (12%)
  between operations  13.8 us (3%)
  starting transfers between devices  5.15 us (1%)
    psum x1, waiting for transfers between devices, local(): total = lax.psum(partial_out, 'tensor')  91.8 us
    psum x2, waiting for transfers between devices, local(): left_sum, right_sum = psum(psum((left_part, right_part), 'tensor'), 'dp')  78.8 us
    all_to_all x1, blocking collectives, local(): lax.all_to_all(clipped_grad, 'tensor', split_axis=0, concat_axis=1, tiled...  52.6 us
    all_to_all x1, waiting for transfers between devices, local(): lax.all_to_all(mixed_grad, 'tensor', split_axis=1, concat_axis=0, tiled=T...  38.1 us
    all_to_all x1, blocking collectives, local(): lax.all_to_all(inputs, 'tensor', split_axis=0, concat_axis=1, tiled=True)  30.3 us
    all_to_all x1, blocking collectives, local(): lax.all_to_all(clipped, 'tensor', split_axis=1, concat_axis=0, tiled=True)  30.1 us
    dot_general x1, matrix products, local(): lax.dot_general(out_grad, weight_rows, (((1,), (1,)), ((), ())), preferre...  19.4 us
    dot_general x1, matrix products, local(): jnp.dot(clipped_back.reshape(tok_rows, -1), weight_rows, preferred_elemen...  18 us
  transfers between devices with their start and end apart: 4, of which 4 were waited for; matrix products, arithmetic and copies ran while one was open for 5% of the time, Pallas kernels for 0%

profile of v1, /device:TPU:8, one launch (start us, length us, event | category | flops | bytes accessed | tf_op | source)
XLA Modules:
  0.0 470.8 jit_solution(11756191320600356570)
XLA Ops:
  7.2 0.0 copy-start
  7.2 0.0 all-reduce.6.cloned.1.call-start
  7.2 2.7 copy.31
  9.9 3.0 copy.32
  12.9 30.3 %all_to_all.69 = bf16[256,16,216]{2,1,0:T(8,128)(2,1)S(1)} all-to-all(bf16[256,16,216]{2,1,0:T(8,128)(2,1)} %copy.32), channel_id=1, replica_groups=mesh['dp'=4,'tensor'=8] {'tensor'}, dimensions={0} | all-to-all | bytes 3538944 | tf_op jit(solution)/shard_map/all_to_all | solution.py:14
  43.2 0.3 copy.33
  43.5 0.0 copy-start.2
  43.5 0.0 copy-start.3
  43.5 0.0 copy-done
  43.5 2.1 fusion.6
  45.7 0.0 copy-done.2
  45.7 0.0 copy-done.3
  45.7 0.0 copy-start.1
  45.7 4.7 multiply_convert_fusion
  50.4 0.0 copy-done.1
  50.4 4.5 copy.36
  54.9 30.1 %all_to_all.70 = bf16[32,128,216]{2,0,1:T(8,128)(2,1)S(1)} all-to-all(bf16[32,128,216]{2,0,1:T(8,128)(2,1)} %copy.36), channel_id=1, replica_groups=mesh['dp'=4,'tensor'=8] {'tensor'}, dimensions={1} | all-to-all | bytes 3538944 | tf_op jit(solution)/shard_map/all_to_all | solution.py:19
  85.0 2.6 copy.38
  87.6 5.2 %reshape.21 = bf16[256,3456]{1,0:T(8,128)(2,1)} reshape(bf16[8,32,16,216]{3,2,1,0:T(8,128)(2,1)} %copy.38) | data formatting | bytes 3538944 | tf_op jit(solution)/shard_map/reshape | solution.py:21
  92.8 18.0 %fusion.12 = f32[256,5120]{1,0:T(8,128)} fusion(bf16[256,3456]{1,0:T(8,128)(2,1)} %reshape.21, bf16[3456,5120]{1,0:T(8,128)(2,1)} %param.10), kind=kOutput, calls=%fused_computation.18 | convolution fusion | flops 9059696640 | bytes 42401792 | tf_op jit(solution)/shard_map/dot_general | solution.py:20
  110.8 0.0 all-reduce.6.cloned.1.call-update
  110.8 91.8 %all-reduce.6.cloned.1.call-done = f32[256,5120]{1,0:T(8,128)} async-done(((f32[256,5120]{1,0:T(8,128)}), f32[256,5120]{1,0:T(8,128)}) %all-reduce.6.cloned.1.call-update) | async-done | bytes 5242896 | tf_op jit(solution)/shard_map/psum | solution.py:23
  202.6 19.4 %fusion.1 = f32[256,3456]{0,1:T(8,128)} fusion(bf16[3456,5120]{1,0:T(8,128)(2,1)} %param.10, f32[256,5120]{1,0:T(8,128)} %all-reduce.6.cloned.1.call-done, bf16[256,5120]{1,0:T(8,128)(2,1)} %param.11), kind=kOutput, calls=%fused_computation.5 | convolution fusion | flops 9063628800 | bytes 46792704 | tf_op jit(solution)/shard_map/dot_general | solution.py:25
  222.0 5.3 %copy.40 = f32[256,16,216]{2,1,0:T(8,128)} copy(f32[256,16,216]{0,2,1:T(8,128)} %bitcast.63) | data formatting | bytes 7077888 | tf_op jit(solution)/shard_map/reshape | solution.py:28
  227.3 52.6 %all_to_all.71 = f32[256,16,216]{2,1,0:T(8,128)S(1)} all-to-all(f32[256,16,216]{2,1,0:T(8,128)} %copy.40), channel_id=1, replica_groups=mesh['dp'=4,'tensor'=8] {'tensor'}, dimensions={0} | all-to-all | bytes 7077888 | tf_op jit(solution)/shard_map/all_to_all | solution.py:29
  279.9 2.7 copy.41
  282.7 5.5 %copy.42 = f32[32,128,216]{1,2,0:T(8,128)} copy(f32[32,128,216]{2,1,0:T(8,128)} %bitcast.55) | data formatting | bytes 7077888 | tf_op jit(solution)/shard_map/all_to_all | solution.py:29
  288.1 6.4 %convolution_bitcast_fusion = f32[32,128,216]{1,2,0:T(8,128)} fusion(f32[32,128,216]{1,2,0:T(8,128)} %copy.42, f32[32,128,216]{1,2,0:T(8,128)} %get-tuple-element.17, f32[128,128]{1,0:T(8,128)S(1)} %copy-done.2), kind=kOutput, calls=%fused_computation.6 | convolution fusion | flops 1361608704 | bytes 10682368 | tf_op jit(solution)/shard_map/jl,tlk->tjk/dot_general | solution.py:31
  294.5 5.2 %copy.43 = f32[32,128,216]{2,0,1:T(8,128)} copy(f32[32,128,216]{1,2,0:T(8,128)} %convolution_bitcast_fusion) | data formatting | bytes 7077888 | tf_op jit(solution)/shard_map/jl,tlk->tjk/transpose | solution.py:31
  299.8 4.5 all-to-all-start.3
  304.3 0.3 all-reduce.8.cloned.1.call-start
  304.6 10.7 %fusion.3 = f32[128,128]{1,0:T(8,128)} fusion(f32[32,128,216]{1,2,0:T(8,128)} %copy-done.1, f32[32,128,216]{1,2,0:T(8,128)} %copy.42, f32[32,128,216]{1,2,0:T(8,128)} %get-tuple-element.17), kind=kOutput, calls=%fused_computation.9 | convolution fusion | flops 1361608704 | bytes 10682368 | tf_op jit(solution)/shard_map/tjk,tlk->jl/dot_general | solution.py:32
  315.3 38.1 %all-to-all-done.3 = f32[32,128,216]{2,0,1:T(8,128)} async-done(((f32[32,128,216]{2,0,1:T(8,128)}), f32[32,128,216]{2,0,1:T(8,128)}, u32[]{:S(2)}, u32[]{:S(2)}) %all-to-all-start.3) | async-done | bytes 3538976 | tf_op jit(solution)/shard_map/all_to_all | solution.py:33
  353.4 6.6 %copy.45 = f32[8,32,16,216]{3,2,1,0:T(8,128)} copy(f32[8,32,16,216]{3,1,2,0:T(8,128)} %bitcast.17) | data formatting | bytes 7077888 | tf_op jit(solution)/shard_map/all_to_all | solution.py:33
  360.0 5.1 %copy.46 = f32[256,16,216]{0,2,1:T(8,128)} copy(f32[256,16,216]{2,1,0:T(8,128)} %bitcast.56) | data formatting | bytes 7077888 | tf_op jit(solution)/shard_map/all_to_all | solution.py:33
  365.1 4.6 convolution_bitcast_fusion.1
  369.6 0.0 all-reduce.8.cloned.1.call-update
  369.7 0.3 all-reduce.10.cloned.1.call-start
  370.0 51.9 %all-reduce.8.cloned.1.call-done = (f32[216,216]{0,1:T(8,128)}, f32[128,128]{1,0:T(8,128)}) async-done(((f32[216,216]{0,1:T(8,128)}, f32[128,128]{1,0:T(8,128)}), (f32[216,216]{0,1:T(8,128)}, f32[128,128]{1,0:T(8,128)})) %all-reduce.8.cloned.1.call-update) | async-done | bytes 252176 | tf_op jit(solution)/shard_map/psum | solution.py:38
  421.8 0.0 all-reduce.10.cloned.1.call-update
  421.9 7.1 %fusion.4 = f32[256,16,216]{0,2,1:T(8,128)} fusion(f32[256,16,216]{0,2,1:T(8,128)} %copy.46, f32[216,216]{1,0:T(8,128)S(1)} %copy-done), kind=kOutput, calls=%fused_computation.10 | convolution fusion | flops 2293235712 | bytes 7264512 | tf_op jit(solution)/shard_map/tjk,ik->tji/dot_general | solution.py:34
  429.0 5.2 %copy.49 = f32[256,3456]{1,0:T(8,128)} copy(f32[256,3456]{0,1:T(8,128)} %bitcast.59) | data formatting | bytes 7077888
  434.1 27.0 %all-reduce.10.cloned.1.call-done = (f32[216,216]{0,1:T(8,128)}, f32[128,128]{1,0:T(8,128)}) async-done(((f32[216,216]{0,1:T(8,128)}, f32[128,128]{1,0:T(8,128)}), (f32[216,216]{0,1:T(8,128)}, f32[128,128]{1,0:T(8,128)})) %all-reduce.10.cloned.1.call-update) | async-done | bytes 252176 | tf_op jit(solution)/shard_map/psum | solution.py:38
  461.1 1.7 copy.48
  462.8 1.5 copy.61
Async XLA Ops:
  7.2 36.4 %copy-start = (f32[216,216]{1,0:T(8,128)S(1)}, f32[216,216]{1,0:T(8,128)}, u32[]{:S(2)}) copy-start(f32[216,216]{1,0:T(8,128)} %param.7) | copy-start | bytes 559876
  7.2 195.4 %all-reduce.6.cloned.1.call-start = ((), (), s32[]{:S(2)}) async-start(), calls=%async_computation.4 | async-start | bytes 10485760 | tf_op jit(solution)/shard_map/psum | solution.py:23
  43.5 2.2 copy-start.2
  43.5 2.2 copy-start.3
  45.7 4.7 copy-start.1
  299.8 53.6 %all-to-all-start.3 = ((f32[32,128,216]{2,0,1:T(8,128)}), f32[32,128,216]{2,0,1:T(8,128)}, u32[]{:S(2)}, u32[]{:S(2)}) async-start(f32[32,128,216]{2,0,1:T(8,128)} %copy.43), calls=%async_computation.3 | async-start | bytes 8388608 | tf_op jit(solution)/shard_map/all_to_all | solution.py:33
  304.3 117.5 %all-reduce.8.cloned.1.call-start = ((), (), s32[]{:S(2)}) async-start(), calls=%async_computation.5 | async-start | bytes 573440 | tf_op jit(solution)/shard_map/psum | solution.py:38
  369.7 91.4 %all-reduce.10.cloned.1.call-start = ((), (), s32[]{:S(2)}) async-start(), calls=%async_computation.6 | async-start | bytes 573440 | tf_op jit(solution)/shard_map/psum | solution.py:38
Sparse Core Ops, SparseCore 0:
  110.9 91.6 all-reduce.5
  369.8 52.0 all-reduce.7
  424.3 36.7 all-reduce.9
